TPU v7x, 128 devices: a whole 4x4x4 slice. The times are simulated.
128 devices in a mesh: row: 8 (over z, core), col: 16 (over y, x).
Axes of the slice: x: 4, y: 4, z: 4, core: 2. Of those that a mesh axis runs over, the one named last changes fastest.
Arguments:
- tiles: float32 [8, 192, 3, 256, 256], P('row', 'col'), may hold values from 0.02 to 1
- slot_tile: int32 [8, 192], P('row', 'col'), may hold values from -1 to 15, as said below
Outputs:
- level_one: float32 [4, 4096, 8192], P(None, 'row', 'col')
- level_two: float32 [4, 2048, 4096], P(None, 'row', 'col')
- level_three: float32 [4, 1024, 2048], P(None, 'row', 'col')
Inputs may be any that keep to these rules, and one draw needn't show every extreme that they name: Slot s of device (i, j) is slot_tile[i, j * 12 + s]. A live slot holds the position p of its tile within the device's 4 x 4 block (tile row p // 4, tile column p % 4); empty slots hold -1. The positions of one device are distinct, its live slots come before its empty ones, a device has 4 to 12 live slots, and in every draw some device has all 12 live. Data in empty slots is not part of the image.
All inputs are finite; a program needn't handle non-finite values.
Results may differ from a plain program's by a relative error of at most 0.0003.
Values sent between devices are 32-bit elements; how exact they have to be, the bound alone decides.
No kernel may reach another device: no remote copies, remote signals or barrier semaphores. Data moves between devices by JAX's collectives and lax.ppermute only.
A program may use at most 128 MiB of HBM per device.

v0:
```python
import jax
import jax.numpy as jnp
import numpy as np
from jax import lax
from jax.experimental import pallas as pl
from jax.experimental.pallas import tpu as pltpu
from jax.sharding import PartitionSpec as P

BR = 4
BC = 4
SLOTS = 12
TILE = 256
WEIGHT_FLOOR = 0.25

ROWS = 544
HALF = 160
INNER = 288
PATCH = 144
TOP = 24
BAND = 18
GROUPS = 7
PACK = 80
XPAD = 24
CPAD = 8
CROWS = 560
ROWS2 = 272


def lanczos(t):
    return np.where(np.abs(t) < 3.0, np.sinc(t) * np.sinc(t / 3.0), 0.0)


SUPPORT = lanczos((np.arange(-5, 7) - 0.5) / 2.0)
NORM = SUPPORT.sum()
TAPS = [float(np.float32(v / NORM)) for v in SUPPORT[5::-1]]


def taper(d):
    return (lanczos((d - 0.5) / 2.0) / NORM).astype(np.float32)


def split(matrix):
    high = matrix.astype(jnp.bfloat16)
    low = (matrix - high.astype(np.float32)).astype(jnp.bfloat16)
    return high, low


def tile_weights():
    x = np.arange(TILE)[:, None]
    lane = np.arange(128)[None, :]
    main = taper(x - 2 * lane)
    spill = np.where(lane < 8, taper(x - 2 * (lane + 128)), np.where(lane >= 120, taper(x - 2 * (lane - 128)), 0.0))
    spill = spill.astype(np.float32)
    mh, ml = split(main)
    sh, sl = split(spill)
    return np.stack([np.concatenate(pair, axis=1) for pair in ((mh, ml), (mh, sh), (sh, sl))])


def opacity_patch():
    x = np.arange(TILE)[None, :]
    rows = taper(x - 2 * np.arange(-8, PATCH - 8)[:, None]).sum(axis=1, dtype=np.float64)
    main = taper(x - 2 * np.arange(128)[:, None]).sum(axis=1, dtype=np.float64)
    lane = np.arange(128)
    right = taper(x - 2 * (lane[:, None] + 128)).sum(axis=1, dtype=np.float64)
    left = taper(x - 2 * (lane[:, None] - 128)).sum(axis=1, dtype=np.float64)
    cols = np.stack([main, np.where(lane >= 64, left, 0.0), np.where(lane < 64, right, 0.0)])
    return (cols[:, None, :] * rows[None, :, None]).astype(np.float32)


def wide_weights(own):
    edge = np.arange(128)
    cols_in = np.concatenate([np.arange(own), np.where(edge < 64, own + edge, edge - 128)])[:, None]
    cols_own = np.arange(own // 2)[None, :]
    cols_edge = np.where(edge < 64, own // 2 + edge, edge - 128)[None, :]
    return taper(cols_in - 2 * cols_own), taper(cols_in - 2 * cols_edge)


def level_two_weights():
    oh, ol = split(wide_weights(512)[0])
    eh, el = split(wide_weights(512)[1])
    th, tl = split(wide_weights(256)[0])
    zero = np.zeros((128, 128), eh.dtype)
    ends = lambda m: np.concatenate([m[:128], m[384:512]])
    beside = lambda *parts: np.concatenate(parts, axis=1)
    rest = [
        ends(oh),
        ends(ol),
        np.concatenate([oh[512:], oh[512:]]),
        np.concatenate([ol[512:], ol[512:]]),
        beside(ends(eh), ends(el)),
        np.concatenate([beside(eh[512:], el[512:]), beside(eh[512:], zero)]),
        beside(th[:256], tl[:256]),
        np.concatenate([beside(th[256:], tl[256:]), beside(th[256:], zero)]),
    ]
    return np.stack([oh[128:384], ol[128:384]]), np.stack(rest)


def fir(load, count, row0):
    rows = {}

    def at(t):
        if t not in rows:
            rows[t] = load(t)
        return rows[t]

    results = []
    for q in range(count):
        total = None
        for k, weight in enumerate(TAPS):
            term = (at(row0 + 2 * q - k) + at(row0 + 2 * q + 1 + k)) * weight
            total = term if total is None else total + term
        results.append(total)
    return results


def halves(value):
    high = value.astype(jnp.bfloat16)
    return high, (value - high.astype(jnp.float32)).astype(jnp.bfloat16)


def split_columns(parts):
    count = len(parts[0])
    highs, lows = [], []
    for q in range(0, count, 2):
        rows = [jnp.concatenate([part[p] for part in parts], axis=1) for p in range(q, min(q + 2, count))]
        high, low = halves(jnp.concatenate(rows, axis=0))
        highs.append(high)
        lows.append(low)
    return jnp.concatenate(highs, axis=0), jnp.concatenate(lows, axis=0)


def dot(left, right):
    return jnp.dot(left, right, preferred_element_type=jnp.float32)


def add_tiles(slot_ref, tiles_ref, weight_ref, patch_ref, canvas_ref, x_ref, v_ref, w_ref, p_ref, list_ref, sem, wsem, outer, before):
    def copies(s, i):
        return [
            pltpu.make_async_copy(
                tiles_ref.at[s, :, :, pl.ds(128 * b, 128)], x_ref.at[i, :, b, pl.ds(XPAD, TILE), :], sem.at[i, b]
            )
            for b in range(2)
        ]

    loads = [pltpu.make_async_copy(weight_ref, w_ref, wsem.at[0]), pltpu.make_async_copy(patch_ref, p_ref, wsem.at[1])]
    count = jnp.int32(0)
    for s in range(SLOTS):
        place = slot_ref[0, s]
        tile_row = place >> 2
        if outer:
            wanted = (place >= 0) & ((tile_row == 0) | (tile_row == BR - 1))
        else:
            wanted = (tile_row == 1) | (tile_row == 2)

        @pl.when(wanted)
        def _(s=s, count=count):
            list_ref[count] = s
            for copy in copies(s, count):
                copy.start()

        count = count + wanted.astype(jnp.int32)
        if s == 0:
            for copy in loads:
                copy.start()

    zero_pad = jnp.zeros((XPAD, 128), jnp.float32)

    def clear_pad(i, carry):
        for c in range(3):
            for b in range(2):
                x_ref[i, c, b, 0:XPAD, :] = zero_pad
                x_ref[i, c, b, XPAD + TILE : 2 * XPAD + TILE, :] = zero_pad
        return carry

    lax.fori_loop(0, count, clear_pad, 0)
    before()
    for copy in loads:
        copy.wait()

    lane = lax.broadcasted_iota(jnp.int32, (1, 128), 1)
    is_left = lane >= 64
    steps = PATCH // 8

    def arrive(i):
        for copy in copies(list_ref[i], i):
            copy.wait()

    def vertical(i):
        for c in range(3):
            parts = [
                fir(lambda t, b=b: x_ref[i, c, b, pl.ds(t, 8, stride=2 * steps), :], steps, XPAD - 16) for b in range(2)
            ]
            v_ref[0, c], v_ref[1, c] = split_columns(parts)

    def horizontal(i):
        place = slot_ref[0, list_ref[i]]
        tile_row = place >> 2
        tile_col = place & 3
        blocks = (tile_col, jnp.where(tile_col == 0, 4, tile_col - 1), tile_col + 1)
        row0 = pl.multiple_of(jnp.where(tile_row == 0, 8, HALF + 8) if outer else tile_row * 128 - 120, 8)

        def add(c, rows, values):
            olds = [[canvas_ref[c, block, r, :] for r in rows] for block in blocks]
            for block, old, new in zip(blocks, olds, values):
                for r, first, second in zip(rows, old, new):
                    canvas_ref[c, block, r, :] = first + second

        for r in range(0, PATCH, 48):
            values = [[p_ref[k, r + t : r + t + 8, :] for t in range(0, 48, 8)] for k in range(3)]
            add(3, [pl.ds(row0 + r + t, 8) for t in range(0, 48, 8)], values)
        for c in range(3):
            first = dot(v_ref[0, c], w_ref[0])
            second = dot(v_ref[1, c], w_ref[1])
            third = dot(v_ref[0, c], w_ref[2])
            main = first[:, :128] + first[:, 128:] + second[:, :128]
            spill = second[:, 128:] + third[:, :128] + third[:, 128:]
            for q0 in range(0, steps, 6):
                mains = [main[8 * q : 8 * q + 8] for q in range(q0, q0 + 6)]
                spills = [spill[8 * q : 8 * q + 8] for q in range(q0, q0 + 6)]
                values = (mains, [jnp.where(is_left, v, 0.0) for v in spills], [jnp.where(is_left, 0.0, v) for v in spills])
                add(c, [pl.ds(row0 + q, 8, stride=steps) for q in range(q0, q0 + 6)], values)

    @pl.when(count > 0)
    def _():
        arrive(0)
        vertical(0)

        def step(i, carry):
            arrive(i)
            horizontal(i - 1)
            vertical(i)
            return carry

        lax.fori_loop(1, count, step, 0)
        horizontal(count - 1)


def clear_canvas(canvas_ref, count):
    zero_rows = jnp.zeros((count // 2, 128), jnp.float32)

    def clear(i, carry):
        c = i // 5
        b = i % 5
        canvas_ref[c, b, 0 : count // 2, :] = zero_rows
        canvas_ref[c, b, count // 2 : count, :] = zero_rows
        return carry

    lax.fori_loop(0, 20, clear, 0)


def outer_kernel(slot_ref, tiles_ref, weight_ref, patch_ref, canvas_ref, up_ref, down_ref, *scratch):
    clear = lambda: clear_canvas(canvas_ref, 2 * HALF)
    add_tiles(slot_ref, tiles_ref, weight_ref, patch_ref, canvas_ref, *scratch, True, clear)
    for c in range(4):
        for b in range(5):
            up_ref[c, b] = canvas_ref[c, b, 8:32, :]
            down_ref[c, b] = canvas_ref[c, b, HALF + 128 : HALF + 152, :]


def inner_kernel(slot_ref, tiles_ref, weight_ref, patch_ref, canvas_ref, *scratch):
    clear = lambda: clear_canvas(canvas_ref, INNER)
    add_tiles(slot_ref, tiles_ref, weight_ref, patch_ref, canvas_ref, *scratch, False, clear)


def canvas_rows(outer_ref, inner_ref, c, b, row, n, kind):
    value = None
    if kind != 2:
        value = outer_ref[c, b, pl.ds(row if kind < 2 else row - (384 - HALF), n), :]
    if kind in (1, 2, 3):
        more = inner_ref[c, b, pl.ds(row - 128, n), :]
        value = more if value is None else value + more
    return value


KINDS = ((0, 128, 0), (128, 160, 1), (160, 384, 2), (384, 416, 3), (416, 544, 4))


def pack_kernel(outer_ref, inner_ref, above_ref, below_ref, left_ref, right_ref):
    lane = lax.broadcasted_iota(jnp.int32, (1, 128), 1)
    is_left = lane >= 64

    def rows_of(c, b, start):
        stop = min(start + PACK, ROWS)
        pieces = []
        for low, high, kind in KINDS:
            first, last = max(low, start), min(high, stop)
            if first < last:
                pieces.append(canvas_rows(outer_ref, inner_ref, c, b, first, last - first, kind))
        value = jnp.concatenate(pieces, axis=0) if len(pieces) > 1 else pieces[0]
        if start == 0:
            value = jnp.concatenate([value[:TOP] + above_ref[c, b], value[TOP:]], axis=0)
        if stop == ROWS:
            value = jnp.concatenate([value[:-TOP], value[-TOP:] + below_ref[c, b]], axis=0)
        return value

    for c in range(4):
        for out_ref, block, first in ((left_ref, 0, 3), (right_ref, 3, 15)):
            packed = None
            for g in range(GROUPS):
                edge, own = rows_of(c, 4, g * PACK), rows_of(c, block, g * PACK)
                band = jnp.where(is_left, edge, own) if block == 0 else jnp.where(is_left, own, edge)
                band = pltpu.roll(band, (first + BAND * g) % 128, 1)
                if packed is None:
                    packed = band
                elif band.shape == packed.shape:
                    packed = jnp.where(lane < BAND * g, packed, band)
                else:
                    rows = band.shape[0]
                    band = jnp.where(lane < BAND * g, packed[:rows], band)
                    packed = jnp.concatenate([band, packed[rows:]], axis=0)
            out_ref[c] = packed


def finish(linear):
    weight = linear[3]
    scale = 1.0 / jnp.maximum(weight, WEIGHT_FLOOR)
    opacity = jnp.clip(weight, 0.0, 1.0)
    colour = [linear[c] * scale for c in range(3)]
    return colour + [opacity], [value * opacity for value in colour] + [opacity]


def level_one_rows(flag_ref, above_ref, below_ref, finish_one, copies):
    has_above, has_below = flag_ref[0], flag_ref[1]

    def run(low, high, kind):
        def body(i, carry):
            row = pl.multiple_of(low + 16 * i, 16)
            finish_one(row, 16, None, 0, None, row - 16, kind)
            return carry

        lax.fori_loop(0, (high - low) // 16, body, 0)

    finish_one(0, 16, above_ref, 0, has_above, None, 0)
    finish_one(16, 8, above_ref, 16, None, 0, 0)
    finish_one(24, 8, None, 0, None, 8, 0)
    run(32, 128, 0)
    run(128, 160, 1)
    run(160, 272, 2)
    for copy in copies[0]:
        copy.start()
    run(272, 384, 2)
    run(384, 416, 3)
    run(416, 512, 4)
    finish_one(512, 8, None, 0, None, 496, 4)
    finish_one(520, 8, below_ref, 0, None, 504, 4)
    for copy in copies[1]:
        copy.start()
    finish_one(528, 16, below_ref, 8, has_below, None, 4)


def clear_carried(carried_ref, blocks):
    zero_pad = jnp.zeros((CPAD, 128), jnp.float32)
    for c in range(4):
        for b in range(blocks):
            carried_ref[c, b, 0:CPAD, :] = zero_pad
            carried_ref[c, b, CPAD + ROWS : CROWS, :] = zero_pad


STEPS2 = ROWS2 // 8
STEPS3 = 17


def middle_kernel(flag_ref, outer_ref, inner_ref, above_ref, below_ref, own_hbm, one_out, part_ref, carried_ref, one_ref, own_ref, sem):
    load = pltpu.make_async_copy(own_hbm, own_ref, sem.at[2])
    load.start()
    clear_carried(carried_ref, 2)

    def finish_one(row, n, band, band_row, mask, out_row, kind):
        for b in range(2):
            linear = []
            for c in range(4):
                value = canvas_rows(outer_ref, inner_ref, c, b + 1, row, n, kind)
                if band is not None:
                    value = value + band[c, b + 1, pl.ds(band_row, n), :]
                if mask is not None:
                    value = value * mask
                linear.append(value)
            shown, carried = finish(linear)
            for c in range(4):
                if out_row is not None:
                    one_ref[c, pl.ds(out_row, n), 128 * b : 128 * b + 128] = shown[c]
                carried_ref[c, b, pl.ds(row + CPAD, n), :] = carried[c]

    copies = [
        [
            pltpu.make_async_copy(
                one_ref.at[:, pl.ds(256 * q, 256), :], one_out.at[:, pl.ds(256 * q, 256), pl.ds(128, 256)], sem.at[q]
            )
        ]
        for q in range(2)
    ]
    level_one_rows(flag_ref, above_ref, below_ref, finish_one, copies)
    load.wait()

    def reduce_two(c, carry):
        parts = [
            fir(lambda t, b=b: carried_ref[c, b, pl.ds(t, 8, stride=2 * STEPS2), :], STEPS2, CPAD) for b in range(2)
        ]
        high, low = split_columns(parts)
        own = dot(high, own_ref[0]) + dot(high, own_ref[1]) + dot(low, own_ref[0])
        part_ref[c, 0] = own[:, :128]
        part_ref[c, 1] = own[:, 128:]
        return carry

    lax.fori_loop(0, 4, reduce_two, 0)
    for pair in copies:
        for copy in pair:
            copy.wait()


def levels_kernel(
    flag_ref, outer_ref, inner_ref, above_ref, below_ref, from_left_ref, from_right_ref, part_ref, own_hbm, one_in,
    one_out, two_out, three_out,
    add_ref, carried_ref, linear_ref, carried2_ref, one_ref, two_ref, three_stage, w_ref, sem,
):
    load = pltpu.make_async_copy(own_hbm, w_ref, sem.at[6])
    load.start()
    has_above, has_below, has_left, has_right = flag_ref[0], flag_ref[1], flag_ref[2], flag_ref[3]
    lane = lax.broadcasted_iota(jnp.int32, (1, 128), 1)
    is_left = lane >= 64
    edge_mask = jnp.where(is_left, has_left, has_right)
    clear_carried(carried_ref, 3)
    for c in range(4):
        for b in range(3):
            carried2_ref[c, b, ROWS2 : ROWS2 + 16, :] = jnp.zeros((16, 128), jnp.float32)

    from_left_lanes = (lane >= 113) | (lane < 3)
    from_right_lanes = (lane >= 125) | (lane < 15)
    for c in range(4):
        for side, ref, first, lanes in ((0, from_left_ref, 15, from_left_lanes), (1, from_right_ref, 3, from_right_lanes)):
            for g in range(GROUPS):
                start, stop = g * PACK, min(g * PACK + PACK, ROWS)
                band = pltpu.roll(ref[c, 0 : stop - start, :], (-first - BAND * g) % 128, 1)
                add_ref[side, c, start:stop, :] = jnp.where(lanes, band, 0.0)

    def finish_one(row, n, band, band_row, mask, out_row, kind):
        rows = pl.ds(row, n)
        for b, block in enumerate((0, 3, 4)):
            linear = []
            for c in range(4):
                value = canvas_rows(outer_ref, inner_ref, c, block, row, n, kind)
                if band is not None:
                    value = value + band[c, block, pl.ds(band_row, n), :]
                if b == 0:
                    value = value + jnp.where(is_left, 0.0, add_ref[0, c, rows, :])
                if b == 1:
                    value = value + jnp.where(is_left, add_ref[1, c, rows, :], 0.0)
                if b == 2:
                    value = value + jnp.where(is_left, add_ref[0, c, rows, :], add_ref[1, c, rows, :])
                    value = value * edge_mask
                if mask is not None:
                    value = value * mask
                linear.append(value)
            shown, carried = finish(linear)
            for c in range(4):
                if b < 2 and out_row is not None:
                    one_ref[b, c, pl.ds(out_row, n), :] = shown[c]
                carried_ref[c, b, pl.ds(row + CPAD, n), :] = carried[c]

    copies = [
        [
            pltpu.make_async_copy(
                one_ref.at[b, :, pl.ds(256 * q, 256), :],
                one_out.at[:, pl.ds(256 * q, 256), pl.ds(384 * b, 128)],
                sem.at[2 * q + b],
            )
            for b in range(2)
        ]
        for q in range(2)
    ]
    level_one_rows(flag_ref, above_ref, below_ref, finish_one, copies)
    load.wait()

    def reduce_two(c, carry):
        parts = [
            fir(lambda t, b=b: carried_ref[c, b, pl.ds(t, 8, stride=2 * STEPS2), :], STEPS2, CPAD) for b in range(3)
        ]
        high, low = split_columns(parts)
        ends, ends_low = high[:, :256], low[:, :256]
        both = jnp.concatenate([high[:, 256:], low[:, 256:]], axis=1)
        own = dot(ends, w_ref[0]) + dot(ends, w_ref[1]) + dot(ends_low, w_ref[0])
        own = own + dot(both, w_ref[2]) + dot(high[:, 256:], w_ref[3, :128, :])
        edge = dot(ends, w_ref[4]) + dot(both, w_ref[5])
        edge = edge[:, :128] + edge[:, 128:] + dot(ends_low, w_ref[4, :, :128])
        own_left = own[:, :128] + part_ref[c, 0]
        own_right = own[:, 128:] + part_ref[c, 1]
        for q in range(STEPS2):
            rows = pl.ds(q, 8, stride=STEPS2)
            linear_ref[c, 0, rows, :] = own_left[8 * q : 8 * q + 8]
            linear_ref[c, 1, rows, :] = own_right[8 * q : 8 * q + 8]
            linear_ref[c, 2, rows, :] = edge[8 * q : 8 * q + 8]
        return carry

    lax.fori_loop(0, 4, reduce_two, 0)

    def finish_two(row, n, mask, out_row):
        rows = pl.ds(row, n)
        for b in range(3):
            linear = []
            for c in range(4):
                value = linear_ref[c, b, rows, :]
                if b == 2:
                    value = value * edge_mask
                if mask is not None:
                    value = value * mask
                linear.append(value)
            shown, carried = finish(linear)
            for c in range(4):
                if b < 2 and out_row is not None:
                    two_ref[c, pl.ds(out_row, n), 128 * b : 128 * b + 128] = shown[c]
                carried2_ref[c, b, rows, :] = carried[c]

    finish_two(0, 8, has_above, None)

    def body_two(i, carry):
        out_row = pl.multiple_of(16 * i, 16)
        finish_two(out_row + 8, 16, None, out_row)
        return carry

    lax.fori_loop(0, 16, body_two, 0)
    finish_two(264, 8, has_below, None)
    two_copy = pltpu.make_async_copy(two_ref, two_out, sem.at[4])
    two_copy.start()

    def reduce_three(c, carry):
        parts = [
            fir(lambda t, b=b: carried2_ref[c, b, pl.ds(t, 8, stride=2 * STEPS3), :], STEPS3, 8) for b in range(3)
        ]
        high, low = split_columns(parts)
        both = jnp.concatenate([high[:, 256:], low[:, 256:]], axis=1)
        total = dot(high[:, :256], w_ref[6]) + dot(both, w_ref[7])
        total = total[:, :128] + total[:, 128:] + dot(low[:, :256], w_ref[6, :, :128])
        for q in range(STEPS3):
            linear_ref[c, 0, pl.ds(q, 8, stride=STEPS3), :] = total[8 * q : 8 * q + 8]
        return carry

    lax.fori_loop(0, 4, reduce_three, 0)
    for row in range(0, 128, 16):
        shown, _ = finish([linear_ref[c, 0, row : row + 16, :] for c in range(4)])
        for c in range(4):
            three_stage[c, row : row + 16, :] = shown[c]
    three_copy = pltpu.make_async_copy(three_stage, three_out, sem.at[5])
    three_copy.start()
    for pair in copies:
        for copy in pair:
            copy.wait()
    two_copy.wait()
    three_copy.wait()


VMEM = pl.BlockSpec(memory_space=pltpu.VMEM)
SMEM = pl.BlockSpec(memory_space=pltpu.SMEM)
HBM = pl.BlockSpec(memory_space=pltpu.HBM)
F32 = jnp.float32
BF16 = jnp.bfloat16


def params(mib):
    return pltpu.CompilerParams(vmem_limit_bytes=mib << 20)


def shifted(value, axis, steps):
    count = lax.axis_size(axis)
    pairs = [(i, i + steps) for i in range(count) if 0 <= i + steps < count]
    return lax.ppermute(value, axis, pairs)


def per_device(tiles, slot_tile):
    shape = jax.ShapeDtypeStruct
    band_shape = pltpu.VMEM((4, 5, TOP, 128), F32)
    pack_shape = pltpu.VMEM((4, PACK, 128), F32)
    in_hbm = lambda value: pltpu.with_memory_space_constraint(value, pltpu.HBM)
    weights, patch = in_hbm(jnp.asarray(tile_weights())), in_hbm(jnp.asarray(opacity_patch()))
    data = in_hbm(tiles[0])
    scratch = [
        pltpu.VMEM((8, 3, 2, TILE + 2 * XPAD, 128), F32),
        pltpu.VMEM((2, 3, PATCH, 256), BF16),
        pltpu.VMEM((3, 256, 256), BF16),
        pltpu.VMEM((3, PATCH, 128), F32),
        pltpu.SMEM((SLOTS,), jnp.int32),
        pltpu.SemaphoreType.DMA((8, 2)),
        pltpu.SemaphoreType.DMA((2,)),
    ]
    outer, up, down = pl.pallas_call(
        outer_kernel,
        name="outer",
        out_shape=(pltpu.VMEM((4, 5, 2 * HALF, 128), F32), band_shape, band_shape),
        in_specs=[SMEM, HBM, HBM, HBM],
        out_specs=(VMEM, VMEM, VMEM),
        scratch_shapes=scratch,
        compiler_params=params(30),
    )(slot_tile, data, weights, patch)
    below = shifted(up, "row", -1)
    above = shifted(down, "row", 1)
    inner = pl.pallas_call(
        inner_kernel,
        name="inner",
        out_shape=pltpu.VMEM((4, 5, INNER, 128), F32),
        in_specs=[SMEM, HBM, HBM, HBM],
        out_specs=VMEM,
        scratch_shapes=scratch,
        cost_estimate=pl.CostEstimate(flops=4_000_000_000, bytes_accessed=4_000_000, transcendentals=0),
        compiler_params=params(30),
    )(slot_tile, data, weights, patch)
    to_left, to_right = pl.pallas_call(
        pack_kernel,
        name="pack",
        out_shape=(pack_shape, pack_shape),
        in_specs=[VMEM] * 4,
        out_specs=(VMEM, VMEM),
        compiler_params=params(20),
    )(outer, inner, above, below)
    from_right = shifted(to_left, "col", -1)
    from_left = shifted(to_right, "col", 1)
    row, col = lax.axis_index("row"), lax.axis_index("col")
    flags = jnp.stack([row > 0, row < lax.axis_size("row") - 1, col > 0, col < lax.axis_size("col") - 1]).astype(F32)
    middle, rest = level_two_weights()
    level_one, part = pl.pallas_call(
        middle_kernel,
        name="middle",
        out_shape=(shape((4, 512, 512), F32), pltpu.VMEM((4, 2, ROWS2, 128), F32)),
        in_specs=[SMEM, VMEM, VMEM, VMEM, VMEM, HBM],
        out_specs=(HBM, VMEM),
        scratch_shapes=[
            pltpu.VMEM((4, 2, CROWS, 128), F32),
            pltpu.VMEM((4, 512, 256), F32),
            pltpu.VMEM((2, 256, 256), BF16),
            pltpu.SemaphoreType.DMA((3,)),
        ],
        cost_estimate=pl.CostEstimate(flops=4_000_000_000, bytes_accessed=4_000_000, transcendentals=0),
        compiler_params=params(30),
    )(flags, outer, inner, above, below, in_hbm(jnp.asarray(middle)))
    return pl.pallas_call(
        levels_kernel,
        name="levels",
        out_shape=(shape((4, 512, 512), F32), shape((4, 256, 256), F32), shape((4, 128, 128), F32)),
        in_specs=[SMEM] + [VMEM] * 7 + [HBM, HBM],
        out_specs=(HBM, HBM, HBM),
        scratch_shapes=[
            pltpu.VMEM((2, 4, ROWS, 128), F32),
            pltpu.VMEM((4, 3, CROWS, 128), F32),
            pltpu.VMEM((4, 3, ROWS2, 128), F32),
            pltpu.VMEM((4, 3, ROWS2 + 16, 128), F32),
            pltpu.VMEM((2, 4, 512, 128), F32),
            pltpu.VMEM((4, 256, 256), F32),
            pltpu.VMEM((4, 128, 128), F32),
            pltpu.VMEM((8, 256, 256), BF16),
            pltpu.SemaphoreType.DMA((7,)),
        ],
        input_output_aliases={9: 0},
        compiler_params=params(30),
    )(flags, outer, inner, above, below, from_left, from_right, part, in_hbm(jnp.asarray(rest)), level_one)


def solution(mesh):
    placed = (P("row", "col", None, None, None), P("row", "col"))
    return jax.shard_map(
        per_device,
        mesh=mesh,
        in_specs=placed,
        out_specs=(P(None, "row", "col"), P(None, "row", "col"), P(None, "row", "col")),
        check_vma=False,
    )
```

profile of v0, /device:TPU:70, one launch (start us, length us, event | category | flops | bytes accessed | tf_op | source)
XLA Modules:
  0.0 40.6 jit_solution(12004594389441595365)
XLA Ops:
  0.6 0.0 copy-start
  0.6 0.6 %copy-done = s32[1,12]{1,0:T(1,128)S(1)} copy-done((s32[1,12]{1,0:T(1,128)S(1)}, s32[1,12]{1,0:T(1,128)}, u32[]{:S(2)}) %copy-start) | copy-done | bytes 72
  1.3 0.0 copy-start.1
  1.3 4.0 %outer.1 = (f32[4,5,320,128]{3,2,1,0:T(8,128)S(1)}, f32[4,5,24,128]{3,2,1,0:T(8,128)}, f32[4,5,24,128]{3,2,1,0:T(8,128)}) custom-call(s32[1,12]{1,0:T(1,128)S(1)} %copy-done, f32[12,3,256,256]{3,2,1,0:T(8,128)} %bitcast.5, bf16[3,256,256]{2,1,0:T(8,128)(2,1)} %constant.23.clone.weight_ref, f32[3,144,128]{2,1,0:T(8,128)} %constant.24.clone.patch_ref), custom_call_target="tpu_custom_call" | custom-call | tf_op jit(solution)/shard_map/outer/pallas_call | solution.py:584
  5.3 3.5 %collective-permute-start = (f32[4,5,24,128]{3,2,1,0:T(8,128)}, f32[4,5,24,128]{3,2,1,0:T(8,128)S(1)}, u32[]{:S(2)}, u32[]{:S(2)}) collective-permute-start(f32[4,5,24,128]{3,2,1,0:T(8,128)} %get-tuple-element.11), channel_id=1, source_target_pairs={{0,16},{16,32},{32,48},{48,64},{64,80},{80,96},{96,112},{1,17},{17... | collective-permute-start | bytes 737288 | tf_op jit(solution)/shard_map/ppermute | solution.py:565
  8.8 2.1 %collective-permute-start.1 = (f32[4,5,24,128]{3,2,1,0:T(8,128)}, f32[4,5,24,128]{3,2,1,0:T(8,128)}, u32[]{:S(2)}, u32[]{:S(2)}) collective-permute-start(f32[4,5,24,128]{3,2,1,0:T(8,128)} %get-tuple-element.12), channel_id=1, source_target_pairs={{16,0},{32,16},{48,32},{64,48},{80,64},{96,80},{112,96},{17,1},{33... | collective-permute-start | bytes 737288 | tf_op jit(solution)/shard_map/ppermute | solution.py:565
  10.9 0.1 add_convert_fusion.flag_ref
  11.0 0.0 copy-done.1
  11.0 3.9 %inner.1.inner_ref = f32[4,5,288,128]{3,2,1,0:T(8,128)S(1)} custom-call(s32[1,12]{1,0:T(1,128)S(1)} %copy-done.1, f32[12,3,256,256]{3,2,1,0:T(8,128)} %bitcast.6, bf16[3,256,256]{2,1,0:T(8,128)(2,1)} %constant.23.clone.weight_ref, f32[3,144,128]{2,1,0:T(8,128)} %constant.24.clone.patch_ref), custom_call_target="tpu_custom_call" | custom-call | flops 4000000000 | bytes 4000000 | tf_op jit(solution)/shard_map/inner/pallas_call | solution.py:595
  14.9 0.0 collective-permute-done.above_ref
  14.9 0.0 collective-permute-done.1.below_ref
  14.9 1.6 %pack.1 = (f32[4,80,128]{2,1,0:T(8,128)S(1)}, f32[4,80,128]{2,1,0:T(8,128)S(1)}) custom-call(f32[4,5,320,128]{3,2,1,0:T(8,128)S(1)} %get-tuple-element.10.outer_ref, f32[4,5,288,128]{3,2,1,0:T(8,128)S(1)} %inner.1.inner_ref, f32[4,5,24,128]{3,2,1,0:T(8,128)S(1)} %collective-permute-done.above_ref, f32[4,5,24,128]{3,2,1,0:T(8,128)} %collective-permute-done.1.below_ref), custom_call_target="tpu_custom_call" | custom-call | tf_op jit(solution)/shard_map/pack/pallas_call | solution.py:605
  16.5 6.7 %collective-permute-start.2 = (f32[4,80,128]{2,1,0:T(8,128)S(1)}, f32[4,80,128]{2,1,0:T(8,128)S(1)}, u32[]{:S(2)}, u32[]{:S(2)}) collective-permute-start(f32[4,80,128]{2,1,0:T(8,128)S(1)} %get-tuple-element.13), channel_id=1, source_target_pairs={{0,1},{1,2},{2,3},{3,4},{4,5},{5,6},{6,7},{7,8},{8,9},{9,10},{10,1... | collective-permute-start | bytes 491528 | tf_op jit(solution)/shard_map/ppermute | solution.py:565
  23.3 1.9 %collective-permute-start.3 = (f32[4,80,128]{2,1,0:T(8,128)S(1)}, f32[4,80,128]{2,1,0:T(8,128)S(1)}, u32[]{:S(2)}, u32[]{:S(2)}) collective-permute-start(f32[4,80,128]{2,1,0:T(8,128)S(1)} %get-tuple-element.14), channel_id=1, source_target_pairs={{1,0},{2,1},{3,2},{4,3},{5,4},{6,5},{7,6},{8,7},{9,8},{10,9},{11,1... | collective-permute-start | bytes 491528 | tf_op jit(solution)/shard_map/ppermute | solution.py:565
  25.2 3.4 %middle.1 = (f32[4,512,512]{2,1,0:T(8,128)}, f32[4,2,272,128]{3,2,1,0:T(8,128)S(1)}) custom-call(f32[4]{0:T(128)S(1)} %add_convert_fusion.flag_ref, f32[4,5,320,128]{3,2,1,0:T(8,128)S(1)} %get-tuple-element.10.outer_ref, f32[4,5,288,128]{3,2,1,0:T(8,128)S(1)} %inner.1.inner_ref, f32[4,5,24,128]{3,2,1,0:T(8,128)S(1)} %collective-permute-done.above_ref, ...), custom_call_target="tpu_custom_call" | custom-call | flops 4000000000 | bytes 4000000 | tf_op jit(solution)/shard_map/middle/pallas_call | solution.py:618
  28.6 0.0 collective-permute-done.2.from_left_ref
  28.6 4.7 %collective-permute-done.3.from_right_ref = f32[4,80,128]{2,1,0:T(8,128)S(1)} collective-permute-done((f32[4,80,128]{2,1,0:T(8,128)S(1)}, f32[4,80,128]{2,1,0:T(8,128)S(1)}, u32[]{:S(2)}, u32[]{:S(2)}) %collective-permute-start.3) | collective-permute-done | bytes 163872 | tf_op jit(solution)/shard_map/ppermute | solution.py:565
  33.4 7.2 %levels.1 = (f32[4,512,512]{2,1,0:T(8,128)}, f32[4,256,256]{2,1,0:T(8,128)}, f32[4,128,128]{2,1,0:T(8,128)}) custom-call(f32[4]{0:T(128)S(1)} %add_convert_fusion.flag_ref, f32[4,5,320,128]{3,2,1,0:T(8,128)S(1)} %get-tuple-element.10.outer_ref, f32[4,5,288,128]{3,2,1,0:T(8,128)S(1)} %inner.1.inner_ref, ...), custom_call_target="tpu_custom_call", output_to_operand_aliasing={{0}: (9, {})} | custom-call | tf_op jit(solution)/shard_map/levels/pallas_call | solution.py:633
Async XLA Ops:
  0.6 0.7 %copy-start = (s32[1,12]{1,0:T(1,128)S(1)}, s32[1,12]{1,0:T(1,128)}, u32[]{:S(2)}) copy-start(s32[1,12]{1,0:T(1,128)} %slot_ref.3) | copy-start | bytes 148
  1.3 9.7 %copy-start.1 = (s32[1,12]{1,0:T(1,128)S(1)}, s32[1,12]{1,0:T(1,128)}, u32[]{:S(2)}) copy-start(s32[1,12]{1,0:T(1,128)} %slot_ref.3) | copy-start | bytes 148
  5.3 9.6 %collective-permute-start = (f32[4,5,24,128]{3,2,1,0:T(8,128)}, f32[4,5,24,128]{3,2,1,0:T(8,128)S(1)}, u32[]{:S(2)}, u32[]{:S(2)}) collective-permute-start(f32[4,5,24,128]{3,2,1,0:T(8,128)} %get-tuple-element.11), channel_id=1, source_target_pairs={{0,16},{16,32},{32,48},{48,64},{64,80},{80,96},{96,112},{1,17},{17... | collective-permute-start | bytes 737288 | tf_op jit(solution)/shard_map/ppermute | solution.py:565
  8.8 6.1 %collective-permute-start.1 = (f32[4,5,24,128]{3,2,1,0:T(8,128)}, f32[4,5,24,128]{3,2,1,0:T(8,128)}, u32[]{:S(2)}, u32[]{:S(2)}) collective-permute-start(f32[4,5,24,128]{3,2,1,0:T(8,128)} %get-tuple-element.12), channel_id=1, source_target_pairs={{16,0},{32,16},{48,32},{64,48},{80,64},{96,80},{112,96},{17,1},{33... | collective-permute-start | bytes 737288 | tf_op jit(solution)/shard_map/ppermute | solution.py:565
  16.5 12.1 %collective-permute-start.2 = (f32[4,80,128]{2,1,0:T(8,128)S(1)}, f32[4,80,128]{2,1,0:T(8,128)S(1)}, u32[]{:S(2)}, u32[]{:S(2)}) collective-permute-start(f32[4,80,128]{2,1,0:T(8,128)S(1)} %get-tuple-element.13), channel_id=1, source_target_pairs={{0,1},{1,2},{2,3},{3,4},{4,5},{5,6},{6,7},{7,8},{8,9},{9,10},{10,1... | collective-permute-start | bytes 491528 | tf_op jit(solution)/shard_map/ppermute | solution.py:565
  23.3 10.1 %collective-permute-start.3 = (f32[4,80,128]{2,1,0:T(8,128)S(1)}, f32[4,80,128]{2,1,0:T(8,128)S(1)}, u32[]{:S(2)}, u32[]{:S(2)}) collective-permute-start(f32[4,80,128]{2,1,0:T(8,128)S(1)} %get-tuple-element.14), channel_id=1, source_target_pairs={{1,0},{2,1},{3,2},{4,3},{5,4},{6,5},{7,6},{8,7},{9,8},{10,9},{11,1... | collective-permute-start | bytes 491528 | tf_op jit(solution)/shard_map/ppermute | solution.py:565
where the time goes:
time: 41 us; the launch traced here: 40.6 us
  Pallas kernels  20.2 us (49%)
  starting transfers between devices  14.2 us (35%)
  waiting for transfers between devices  4.75 us (12%)
  between operations  0.73 us (2%)
  local copies, waits for them, and re-layouts  0.65 us (2%)
    ppermute x4, starting transfers between devices, shifted(): return lax.ppermute(value, axis, pairs)  14.2 us
    pallas_call x1, Pallas kernels, per_device(): pl.pallas_call(levels_kernel, name='levels', out_shape=(shape((4, 512, 51...  7.24 us
    ppermute x4, waiting for transfers between devices, shifted(): return lax.ppermute(value, axis, pairs)  4.75 us
    pallas_call x1, Pallas kernels, per_device(): pl.pallas_call(outer_kernel, name='outer', out_shape=(pltpu.VMEM((4, 5, 2...  4.05 us
    pallas_call x1, Pallas kernels, per_device(): pl.pallas_call(inner_kernel, name='inner', out_shape=pltpu.VMEM((4, 5, IN...  3.87 us
    pallas_call x1, Pallas kernels, per_device(): pl.pallas_call(middle_kernel, name='middle', out_shape=(shape((4, 512, 51...  3.41 us
    pallas_call x1, Pallas kernels, per_device(): pl.pallas_call(pack_kernel, name='pack', out_shape=(pack_shape, pack_shap...  1.6 us
  transfers between devices with their start and end apart: 4, of which 1 were waited for; matrix products, arithmetic and copies ran while one was open for 0% of the time, Pallas kernels for 18%

commit v1 on v0

--- a/solution.py
+++ b/solution.py
@@ -13,8 +13,8 @@
 WEIGHT_FLOOR = 0.25
 
 ROWS = 544
-HALF = 160
 INNER = 288
+QUOTA = 8
 PATCH = 144
 TOP = 24
 BAND = 18
@@ -133,7 +133,7 @@
     return jnp.dot(left, right, preferred_element_type=jnp.float32)
 
 
-def add_tiles(slot_ref, tiles_ref, weight_ref, patch_ref, canvas_ref, x_ref, v_ref, w_ref, p_ref, list_ref, sem, wsem, outer, before):
+def add_tiles(slot_hbm, tiles_ref, weight_ref, patch_ref, canvas_ref, x_ref, v_ref, w_ref, p_ref, slot_ref, list_ref, sem, wsem, outer):
     def copies(s, i):
         return [
             pltpu.make_async_copy(
@@ -143,26 +143,8 @@
         ]
 
     loads = [pltpu.make_async_copy(weight_ref, w_ref, wsem.at[0]), pltpu.make_async_copy(patch_ref, p_ref, wsem.at[1])]
-    count = jnp.int32(0)
-    for s in range(SLOTS):
-        place = slot_ref[0, s]
-        tile_row = place >> 2
-        if outer:
-            wanted = (place >= 0) & ((tile_row == 0) | (tile_row == BR - 1))
-        else:
-            wanted = (tile_row == 1) | (tile_row == 2)
-
-        @pl.when(wanted)
-        def _(s=s, count=count):
-            list_ref[count] = s
-            for copy in copies(s, count):
-                copy.start()
-
-        count = count + wanted.astype(jnp.int32)
-        if s == 0:
-            for copy in loads:
-                copy.start()
-
+    slots = pltpu.make_async_copy(slot_hbm, slot_ref, wsem.at[2])
+    slots.start()
     zero_pad = jnp.zeros((XPAD, 128), jnp.float32)
 
     def clear_pad(i, carry):
@@ -172,8 +154,42 @@
                 x_ref[i, c, b, XPAD + TILE : 2 * XPAD + TILE, :] = zero_pad
         return carry
 
-    lax.fori_loop(0, count, clear_pad, 0)
-    before()
+    lax.fori_loop(0, 8, clear_pad, 0)
+    slots.wait()
+    count = jnp.int32(0)
+    places = [slot_ref[0, s] for s in range(SLOTS)]
+    at_edge = [(place >= 0) & (((place >> 2) == 0) | ((place >> 2) == BR - 1)) for place in places]
+    in_middle = [((place >> 2) == 1) | ((place >> 2) == 2) for place in places]
+    edges = jnp.int32(0)
+    for flag in at_edge:
+        edges = edges + flag.astype(jnp.int32)
+    spare = QUOTA - edges
+
+    def take(s, wanted, count):
+        @pl.when(wanted)
+        def _():
+            list_ref[count] = s
+            for copy in copies(s, count):
+                copy.start()
+
+        return count + wanted.astype(jnp.int32)
+
+    if outer:
+        for s in range(SLOTS):
+            count = take(s, at_edge[s], count)
+            if s == 3:
+                for copy in loads:
+                    copy.start()
+    seen = jnp.int32(0)
+    for s in range(SLOTS):
+        wanted = in_middle[s] & ((seen < spare) if outer else (seen >= spare))
+        count = take(s, wanted, count)
+        seen = seen + in_middle[s].astype(jnp.int32)
+        if s == 3 and not outer:
+            for copy in loads:
+                copy.start()
+
+    clear_canvas(canvas_ref, ROWS if outer else INNER)
     for copy in loads:
         copy.wait()
 
@@ -197,7 +213,7 @@
         tile_row = place >> 2
         tile_col = place & 3
         blocks = (tile_col, jnp.where(tile_col == 0, 4, tile_col - 1), tile_col + 1)
-        row0 = pl.multiple_of(jnp.where(tile_row == 0, 8, HALF + 8) if outer else tile_row * 128 - 120, 8)
+        row0 = pl.multiple_of(tile_row * 128 + (8 if outer else -120), 8)
 
         def add(c, rows, values):
             olds = [[canvas_ref[c, block, r, :] for r in rows] for block in blocks]
@@ -249,33 +265,29 @@
 
 
 def outer_kernel(slot_ref, tiles_ref, weight_ref, patch_ref, canvas_ref, up_ref, down_ref, *scratch):
-    clear = lambda: clear_canvas(canvas_ref, 2 * HALF)
-    add_tiles(slot_ref, tiles_ref, weight_ref, patch_ref, canvas_ref, *scratch, True, clear)
+    add_tiles(slot_ref, tiles_ref, weight_ref, patch_ref, canvas_ref, *scratch, True)
     for c in range(4):
         for b in range(5):
             up_ref[c, b] = canvas_ref[c, b, 8:32, :]
-            down_ref[c, b] = canvas_ref[c, b, HALF + 128 : HALF + 152, :]
+            down_ref[c, b] = canvas_ref[c, b, 512:536, :]
 
 
 def inner_kernel(slot_ref, tiles_ref, weight_ref, patch_ref, canvas_ref, *scratch):
-    clear = lambda: clear_canvas(canvas_ref, INNER)
-    add_tiles(slot_ref, tiles_ref, weight_ref, patch_ref, canvas_ref, *scratch, False, clear)
+    add_tiles(slot_ref, tiles_ref, weight_ref, patch_ref, canvas_ref, *scratch, False)
 
 
 def canvas_rows(outer_ref, inner_ref, c, b, row, n, kind):
-    value = None
-    if kind != 2:
-        value = outer_ref[c, b, pl.ds(row if kind < 2 else row - (384 - HALF), n), :]
-    if kind in (1, 2, 3):
-        more = inner_ref[c, b, pl.ds(row - 128, n), :]
-        value = more if value is None else value + more
-    return value
-
-
-KINDS = ((0, 128, 0), (128, 160, 1), (160, 384, 2), (384, 416, 3), (416, 544, 4))
-
-
-def pack_kernel(outer_ref, inner_ref, above_ref, below_ref, left_ref, right_ref):
+    value = outer_ref[c, b, pl.ds(row, n), :]
+    return value + inner_ref[c, b, pl.ds(row - 128, n), :] if kind else value
+
+
+KINDS = ((0, 128, 0), (128, 416, 1), (416, ROWS, 0))
+
+
+def pack_kernel(outer_ref, inner_ref, above_any, below_any, left_ref, right_ref, top_ref, bottom_ref, band_ref, sem):
+    bands = [pltpu.make_async_copy(ref, band_ref.at[k], sem.at[k]) for k, ref in enumerate((above_any, below_any))]
+    for copy in bands:
+        copy.start()
     lane = lax.broadcasted_iota(jnp.int32, (1, 128), 1)
     is_left = lane >= 64
 
@@ -288,27 +300,38 @@
                 pieces.append(canvas_rows(outer_ref, inner_ref, c, b, first, last - first, kind))
         value = jnp.concatenate(pieces, axis=0) if len(pieces) > 1 else pieces[0]
         if start == 0:
-            value = jnp.concatenate([value[:TOP] + above_ref[c, b], value[TOP:]], axis=0)
+            value = jnp.concatenate([top_ref[c, b], value[TOP:]], axis=0)
         if stop == ROWS:
-            value = jnp.concatenate([value[:-TOP], value[-TOP:] + below_ref[c, b]], axis=0)
+            value = jnp.concatenate([value[:-TOP], bottom_ref[c, b]], axis=0)
         return value
 
-    for c in range(4):
-        for out_ref, block, first in ((left_ref, 0, 3), (right_ref, 3, 15)):
-            packed = None
-            for g in range(GROUPS):
-                edge, own = rows_of(c, 4, g * PACK), rows_of(c, block, g * PACK)
-                band = jnp.where(is_left, edge, own) if block == 0 else jnp.where(is_left, own, edge)
-                band = pltpu.roll(band, (first + BAND * g) % 128, 1)
-                if packed is None:
-                    packed = band
-                elif band.shape == packed.shape:
-                    packed = jnp.where(lane < BAND * g, packed, band)
-                else:
-                    rows = band.shape[0]
-                    band = jnp.where(lane < BAND * g, packed[:rows], band)
-                    packed = jnp.concatenate([band, packed[rows:]], axis=0)
-            out_ref[c] = packed
+    def packed(c, block, first, groups, start):
+        for g in groups:
+            edge, own = rows_of(c, 4, g * PACK), rows_of(c, block, g * PACK)
+            band = jnp.where(is_left, edge, own) if block == 0 else jnp.where(is_left, own, edge)
+            band = pltpu.roll(band, (first + BAND * g) % 128, 1)
+            if start is None:
+                start = band
+                continue
+            rows = band.shape[0]
+            mask = (lane >= BAND * g) & (lane < BAND * (g + 1))
+            head = jnp.where(mask, band, start[:rows])
+            start = head if rows == PACK else jnp.concatenate([head, start[rows:]], axis=0)
+        return start
+
+    sides = ((left_ref, 0, 3), (right_ref, 3, 15))
+    for c in range(4):
+        for out_ref, block, first in sides:
+            out_ref[c] = packed(c, block, first, range(1, GROUPS - 1), None)
+    for copy in bands:
+        copy.wait()
+    for c in range(4):
+        for b in range(5):
+            top_ref[c, b] = outer_ref[c, b, 0:TOP, :] + band_ref[0, c, b]
+            bottom_ref[c, b] = outer_ref[c, b, ROWS - TOP : ROWS, :] + band_ref[1, c, b]
+    for c in range(4):
+        for out_ref, block, first in sides:
+            out_ref[c] = packed(c, block, first, (0, GROUPS - 1), out_ref[c])
 
 
 def finish(linear):
@@ -319,8 +342,14 @@
     return colour + [opacity], [value * opacity for value in colour] + [opacity]
 
 
-def level_one_rows(flag_ref, above_ref, below_ref, finish_one, copies):
-    has_above, has_below = flag_ref[0], flag_ref[1]
+def neighbours():
+    row, col = lax.axis_index("row"), lax.axis_index("col")
+    found = (row > 0, row < lax.axis_size("row") - 1, col > 0, col < lax.axis_size("col") - 1)
+    return [jnp.where(flag, 1.0, 0.0).astype(jnp.float32) for flag in found]
+
+
+def level_one_rows(top_ref, bottom_ref, finish_one, copies):
+    has_above, has_below, _, _ = neighbours()
 
     def run(low, high, kind):
         def body(i, carry):
@@ -330,22 +359,20 @@
 
         lax.fori_loop(0, (high - low) // 16, body, 0)
 
-    finish_one(0, 16, above_ref, 0, has_above, None, 0)
-    finish_one(16, 8, above_ref, 16, None, 0, 0)
+    finish_one(0, 16, top_ref, 0, has_above, None, 0)
+    finish_one(16, 8, top_ref, 16, None, 0, 0)
     finish_one(24, 8, None, 0, None, 8, 0)
     run(32, 128, 0)
-    run(128, 160, 1)
-    run(160, 272, 2)
+    run(128, 272, 1)
     for copy in copies[0]:
         copy.start()
-    run(272, 384, 2)
-    run(384, 416, 3)
-    run(416, 512, 4)
-    finish_one(512, 8, None, 0, None, 496, 4)
-    finish_one(520, 8, below_ref, 0, None, 504, 4)
+    run(272, 416, 1)
+    run(416, 512, 0)
+    finish_one(512, 8, None, 0, None, 496, 0)
+    finish_one(520, 8, bottom_ref, 0, None, 504, 0)
     for copy in copies[1]:
         copy.start()
-    finish_one(528, 16, below_ref, 8, has_below, None, 4)
+    finish_one(528, 16, bottom_ref, 8, has_below, None, 0)
 
 
 def clear_carried(carried_ref, blocks):
@@ -360,7 +387,7 @@
 STEPS3 = 17
 
 
-def middle_kernel(flag_ref, outer_ref, inner_ref, above_ref, below_ref, own_hbm, one_out, part_ref, carried_ref, one_ref, own_ref, sem):
+def middle_kernel(outer_ref, inner_ref, top_ref, bottom_ref, own_hbm, one_out, part_ref, carried_ref, one_ref, own_ref, sem):
     load = pltpu.make_async_copy(own_hbm, own_ref, sem.at[2])
     load.start()
     clear_carried(carried_ref, 2)
@@ -369,9 +396,10 @@
         for b in range(2):
             linear = []
             for c in range(4):
-                value = canvas_rows(outer_ref, inner_ref, c, b + 1, row, n, kind)
-                if band is not None:
-                    value = value + band[c, b + 1, pl.ds(band_row, n), :]
+                if band is None:
+                    value = canvas_rows(outer_ref, inner_ref, c, b + 1, row, n, kind)
+                else:
+                    value = band[c, b + 1, pl.ds(band_row, n), :]
                 if mask is not None:
                     value = value * mask
                 linear.append(value)
@@ -389,7 +417,7 @@
         ]
         for q in range(2)
     ]
-    level_one_rows(flag_ref, above_ref, below_ref, finish_one, copies)
+    level_one_rows(top_ref, bottom_ref, finish_one, copies)
     load.wait()
 
     def reduce_two(c, carry):
@@ -402,20 +430,21 @@
         part_ref[c, 1] = own[:, 128:]
         return carry
 
-    lax.fori_loop(0, 4, reduce_two, 0)
+    for c in range(4):
+        reduce_two(c, 0)
     for pair in copies:
         for copy in pair:
             copy.wait()
 
 
 def levels_kernel(
-    flag_ref, outer_ref, inner_ref, above_ref, below_ref, from_left_ref, from_right_ref, part_ref, own_hbm, one_in,
+    outer_ref, inner_ref, top_ref, bottom_ref, from_left_ref, from_right_ref, part_ref, own_hbm, one_in,
     one_out, two_out, three_out,
     add_ref, carried_ref, linear_ref, carried2_ref, one_ref, two_ref, three_stage, w_ref, sem,
 ):
     load = pltpu.make_async_copy(own_hbm, w_ref, sem.at[6])
     load.start()
-    has_above, has_below, has_left, has_right = flag_ref[0], flag_ref[1], flag_ref[2], flag_ref[3]
+    has_above, has_below, has_left, has_right = neighbours()
     lane = lax.broadcasted_iota(jnp.int32, (1, 128), 1)
     is_left = lane >= 64
     edge_mask = jnp.where(is_left, has_left, has_right)
@@ -438,9 +467,10 @@
         for b, block in enumerate((0, 3, 4)):
             linear = []
             for c in range(4):
-                value = canvas_rows(outer_ref, inner_ref, c, block, row, n, kind)
-                if band is not None:
-                    value = value + band[c, block, pl.ds(band_row, n), :]
+                if band is None:
+                    value = canvas_rows(outer_ref, inner_ref, c, block, row, n, kind)
+                else:
+                    value = band[c, block, pl.ds(band_row, n), :]
                 if b == 0:
                     value = value + jnp.where(is_left, 0.0, add_ref[0, c, rows, :])
                 if b == 1:
@@ -468,7 +498,7 @@
         ]
         for q in range(2)
     ]
-    level_one_rows(flag_ref, above_ref, below_ref, finish_one, copies)
+    level_one_rows(top_ref, bottom_ref, finish_one, copies)
     load.wait()
 
     def reduce_two(c, carry):
@@ -491,7 +521,8 @@
             linear_ref[c, 2, rows, :] = edge[8 * q : 8 * q + 8]
         return carry
 
-    lax.fori_loop(0, 4, reduce_two, 0)
+    for c in range(4):
+        reduce_two(c, 0)
 
     def finish_two(row, n, mask, out_row):
         rows = pl.ds(row, n)
@@ -534,7 +565,8 @@
             linear_ref[c, 0, pl.ds(q, 8, stride=STEPS3), :] = total[8 * q : 8 * q + 8]
         return carry
 
-    lax.fori_loop(0, 4, reduce_three, 0)
+    for c in range(4):
+        reduce_three(c, 0)
     for row in range(0, 128, 16):
         shown, _ = finish([linear_ref[c, 0, row : row + 16, :] for c in range(4)])
         for c in range(4):
@@ -549,8 +581,8 @@
 
 
 VMEM = pl.BlockSpec(memory_space=pltpu.VMEM)
-SMEM = pl.BlockSpec(memory_space=pltpu.SMEM)
 HBM = pl.BlockSpec(memory_space=pltpu.HBM)
+ANY = pl.BlockSpec(memory_space=pl.ANY)
 F32 = jnp.float32
 BF16 = jnp.bfloat16
 
@@ -571,55 +603,55 @@
     pack_shape = pltpu.VMEM((4, PACK, 128), F32)
     in_hbm = lambda value: pltpu.with_memory_space_constraint(value, pltpu.HBM)
     weights, patch = in_hbm(jnp.asarray(tile_weights())), in_hbm(jnp.asarray(opacity_patch()))
-    data = in_hbm(tiles[0])
+    data, slots = in_hbm(tiles[0]), in_hbm(slot_tile)
     scratch = [
         pltpu.VMEM((8, 3, 2, TILE + 2 * XPAD, 128), F32),
         pltpu.VMEM((2, 3, PATCH, 256), BF16),
         pltpu.VMEM((3, 256, 256), BF16),
         pltpu.VMEM((3, PATCH, 128), F32),
+        pltpu.SMEM((1, SLOTS), jnp.int32),
         pltpu.SMEM((SLOTS,), jnp.int32),
         pltpu.SemaphoreType.DMA((8, 2)),
-        pltpu.SemaphoreType.DMA((2,)),
+        pltpu.SemaphoreType.DMA((3,)),
     ]
     outer, up, down = pl.pallas_call(
         outer_kernel,
         name="outer",
-        out_shape=(pltpu.VMEM((4, 5, 2 * HALF, 128), F32), band_shape, band_shape),
-        in_specs=[SMEM, HBM, HBM, HBM],
+        out_shape=(pltpu.VMEM((4, 5, ROWS, 128), F32), band_shape, band_shape),
+        in_specs=[HBM] * 4,
         out_specs=(VMEM, VMEM, VMEM),
         scratch_shapes=scratch,
         compiler_params=params(30),
-    )(slot_tile, data, weights, patch)
+    )(slots, data, weights, patch)
     below = shifted(up, "row", -1)
     above = shifted(down, "row", 1)
     inner = pl.pallas_call(
         inner_kernel,
         name="inner",
         out_shape=pltpu.VMEM((4, 5, INNER, 128), F32),
-        in_specs=[SMEM, HBM, HBM, HBM],
+        in_specs=[HBM] * 4,
         out_specs=VMEM,
         scratch_shapes=scratch,
         cost_estimate=pl.CostEstimate(flops=4_000_000_000, bytes_accessed=4_000_000, transcendentals=0),
         compiler_params=params(30),
-    )(slot_tile, data, weights, patch)
-    to_left, to_right = pl.pallas_call(
+    )(slots, data, weights, patch)
+    to_left, to_right, top, bottom = pl.pallas_call(
         pack_kernel,
         name="pack",
-        out_shape=(pack_shape, pack_shape),
-        in_specs=[VMEM] * 4,
-        out_specs=(VMEM, VMEM),
+        out_shape=(pack_shape, pack_shape, band_shape, band_shape),
+        in_specs=[VMEM, VMEM, ANY, ANY],
+        out_specs=(VMEM,) * 4,
+        scratch_shapes=[pltpu.VMEM((2, 4, 5, TOP, 128), F32), pltpu.SemaphoreType.DMA((2,))],
         compiler_params=params(20),
     )(outer, inner, above, below)
     from_right = shifted(to_left, "col", -1)
     from_left = shifted(to_right, "col", 1)
-    row, col = lax.axis_index("row"), lax.axis_index("col")
-    flags = jnp.stack([row > 0, row < lax.axis_size("row") - 1, col > 0, col < lax.axis_size("col") - 1]).astype(F32)
     middle, rest = level_two_weights()
     level_one, part = pl.pallas_call(
         middle_kernel,
         name="middle",
         out_shape=(shape((4, 512, 512), F32), pltpu.VMEM((4, 2, ROWS2, 128), F32)),
-        in_specs=[SMEM, VMEM, VMEM, VMEM, VMEM, HBM],
+        in_specs=[VMEM, VMEM, VMEM, VMEM, HBM],
         out_specs=(HBM, VMEM),
         scratch_shapes=[
             pltpu.VMEM((4, 2, CROWS, 128), F32),
@@ -629,12 +661,12 @@
         ],
         cost_estimate=pl.CostEstimate(flops=4_000_000_000, bytes_accessed=4_000_000, transcendentals=0),
         compiler_params=params(30),
-    )(flags, outer, inner, above, below, in_hbm(jnp.asarray(middle)))
+    )(outer, inner, top, bottom, in_hbm(jnp.asarray(middle)))
     return pl.pallas_call(
         levels_kernel,
         name="levels",
         out_shape=(shape((4, 512, 512), F32), shape((4, 256, 256), F32), shape((4, 128, 128), F32)),
-        in_specs=[SMEM] + [VMEM] * 7 + [HBM, HBM],
+        in_specs=[VMEM] * 7 + [HBM, HBM],
         out_specs=(HBM, HBM, HBM),
         scratch_shapes=[
             pltpu.VMEM((2, 4, ROWS, 128), F32),
@@ -647,9 +679,9 @@
             pltpu.VMEM((8, 256, 256), BF16),
             pltpu.SemaphoreType.DMA((7,)),
         ],
-        input_output_aliases={9: 0},
+        input_output_aliases={8: 0},
         compiler_params=params(30),
-    )(flags, outer, inner, above, below, from_left, from_right, part, in_hbm(jnp.asarray(rest)), level_one)
+    )(outer, inner, top, bottom, from_left, from_right, part, in_hbm(jnp.asarray(rest)), level_one)
 
 
 def solution(mesh):

time: 41 us -> 39.2 us (0.956)
  waiting for transfers between devices: 4.75 us -> 8.57 us
  Pallas kernels: 20.2 us -> 17 us
  starting transfers between devices: 14.2 us -> 12.8 us
  local copies, waits for them, and re-layouts: 0.65 us -> 0 us
    ppermute x4, waiting for transfers between devices: 4.75 us -> 8.57 us  [shifted(): return lax.ppermute(value, axis, pairs)]
    pallas_call x1, Pallas kernels: 3.87 us -> 2.03 us  [per_device(): pl.pallas_call(inner_kernel, name='inner', out_shape=pltpu.VMEM((4, 5, IN...]
    pallas_call x1, Pallas kernels: 4.05 us -> 5.65 us  [per_device(): pl.pallas_call(outer_kernel, name='outer', out_shape=(pltpu.VMEM((4, 5, R...]
    pallas_call x1, Pallas kernels: 7.24 us -> 5.78 us  [per_device(): pl.pallas_call(levels_kernel, name='levels', out_shape=(shape((4, 512, 51...]
    ppermute x4, starting transfers between devices: 14.2 us -> 12.8 us  [shifted(): return lax.ppermute(value, axis, pairs)]
    pallas_call x1, Pallas kernels: 3.41 us -> 2.17 us  [per_device(): pl.pallas_call(middle_kernel, name='middle', out_shape=(shape((4, 512, 51...]
    unnamed x4 -> x0, local copies, waits for them, and re-layouts: 0.65 us -> none
  transfers between devices with their start and end apart: 4 -> 4, of which waited for: 1 -> 3; matrix products, arithmetic and copies ran while one was open for 0% -> 0% of each run, Pallas kernels for 18% -> 11%
where the time goes in v1:
time: 39.2 us; the launch traced here: 39.1 us
  Pallas kernels  17 us (43%)
  starting transfers between devices  12.8 us (33%)
  waiting for transfers between devices  8.57 us (22%)
  between operations  0.7 us (2%)
    ppermute x4, starting transfers between devices, shifted(): return lax.ppermute(value, axis, pairs)  12.8 us
    ppermute x4, waiting for transfers between devices, shifted(): return lax.ppermute(value, axis, pairs)  8.57 us
    pallas_call x1, Pallas kernels, per_device(): pl.pallas_call(levels_kernel, name='levels', out_shape=(shape((4, 512, 51...  5.78 us
    pallas_call x1, Pallas kernels, per_device(): pl.pallas_call(outer_kernel, name='outer', out_shape=(pltpu.VMEM((4, 5, R...  5.65 us
    pallas_call x1, Pallas kernels, per_device(): pl.pallas_call(middle_kernel, name='middle', out_shape=(shape((4, 512, 51...  2.17 us
    pallas_call x1, Pallas kernels, per_device(): pl.pallas_call(inner_kernel, name='inner', out_shape=pltpu.VMEM((4, 5, IN...  2.03 us
    pallas_call x1, Pallas kernels, per_device(): pl.pallas_call(pack_kernel, name='pack', out_shape=(pack_shape, pack_shap...  1.38 us
  transfers between devices with their start and end apart: 4, of which 3 were waited for; matrix products, arithmetic and copies ran while one was open for 0% of the time, Pallas kernels for 11%

profile of v1, /device:TPU:70, one launch (start us, length us, event | category | flops | bytes accessed | tf_op | source)
XLA Modules:
  0.0 39.1 jit_solution(793221663894989909)
XLA Ops:
  0.6 5.6 %outer.1 = (f32[4,5,544,128]{3,2,1,0:T(8,128)S(1)}, f32[4,5,24,128]{3,2,1,0:T(8,128)S(1)}, f32[4,5,24,128]{3,2,1,0:T(8,128)S(1)}) custom-call(s32[1,12]{1,0:T(1,128)} %slot_ref.3, f32[12,3,256,256]{3,2,1,0:T(8,128)} %bitcast.1, bf16[3,256,256]{2,1,0:T(8,128)(2,1)} %constant.8.clone.weight_ref, f32[3,144,128]{2,1,0:T(8,128)} %constant.9.clone.patch_ref), custom_call_target="tpu_custom_call" | custom-call | tf_op jit(solution)/shard_map/outer/pallas_call | solution.py:617
  6.3 2.9 %collective-permute-start = (f32[4,5,24,128]{3,2,1,0:T(8,128)S(1)}, f32[4,5,24,128]{3,2,1,0:T(8,128)S(1)}, u32[]{:S(2)}, u32[]{:S(2)}) collective-permute-start(f32[4,5,24,128]{3,2,1,0:T(8,128)S(1)} %get-tuple-element.13), channel_id=1, source_target_pairs={{0,16},{16,32},{32,48},{48,64},{64,80},{80,96},{96,112},{1,17},{17... | collective-permute-start | bytes 737288 | tf_op jit(solution)/shard_map/ppermute | solution.py:597
  9.2 2.6 %collective-permute-start.1 = (f32[4,5,24,128]{3,2,1,0:T(8,128)S(1)}, f32[4,5,24,128]{3,2,1,0:T(8,128)S(1)}, u32[]{:S(2)}, u32[]{:S(2)}) collective-permute-start(f32[4,5,24,128]{3,2,1,0:T(8,128)S(1)} %get-tuple-element.14), channel_id=1, source_target_pairs={{16,0},{32,16},{48,32},{64,48},{80,64},{96,80},{112,96},{17,1},{33... | collective-permute-start | bytes 737288 | tf_op jit(solution)/shard_map/ppermute | solution.py:597
  11.9 2.0 %inner.1.inner_ref = f32[4,5,288,128]{3,2,1,0:T(8,128)S(1)} custom-call(s32[1,12]{1,0:T(1,128)} %slot_ref.3, f32[12,3,256,256]{3,2,1,0:T(8,128)} %bitcast.2, bf16[3,256,256]{2,1,0:T(8,128)(2,1)} %constant.8.clone.weight_ref, f32[3,144,128]{2,1,0:T(8,128)} %constant.9.clone.patch_ref), custom_call_target="tpu_custom_call" | custom-call | flops 4000000000 | bytes 4000000 | tf_op jit(solution)/shard_map/inner/pallas_call | solution.py:628
  13.9 0.0 collective-permute-done.above_any
  13.9 1.6 %collective-permute-done.1.below_any = f32[4,5,24,128]{3,2,1,0:T(8,128)S(1)} collective-permute-done((f32[4,5,24,128]{3,2,1,0:T(8,128)S(1)}, f32[4,5,24,128]{3,2,1,0:T(8,128)S(1)}, u32[]{:S(2)}, u32[]{:S(2)}) %collective-permute-start.1) | collective-permute-done | bytes 245792 | tf_op jit(solution)/shard_map/ppermute | solution.py:597
  15.6 1.4 %pack.1 = (f32[4,80,128]{2,1,0:T(8,128)S(1)}, f32[4,80,128]{2,1,0:T(8,128)S(1)}, f32[4,5,24,128]{3,2,1,0:T(8,128)S(1)}, f32[4,5,24,128]{3,2,1,0:T(8,128)S(1)}) custom-call(f32[4,5,544,128]{3,2,1,0:T(8,128)S(1)} %get-tuple-element.12.outer_ref, f32[4,5,288,128]{3,2,1,0:T(8,128)S(1)} %inner.1.inner_ref, f32[4,5,24,128]{3,2,1,0:T(8,128)S(1)} %collective-permute-done.above_any, ...), custom_call_target="tpu_custom_call" | custom-call | tf_op jit(solution)/shard_map/pack/pallas_call | solution.py:638
  16.9 5.3 %collective-permute-start.2 = (f32[4,80,128]{2,1,0:T(8,128)S(1)}, f32[4,80,128]{2,1,0:T(8,128)S(1)}, u32[]{:S(2)}, u32[]{:S(2)}) collective-permute-start(f32[4,80,128]{2,1,0:T(8,128)S(1)} %get-tuple-element.17), channel_id=1, source_target_pairs={{0,1},{1,2},{2,3},{3,4},{4,5},{5,6},{6,7},{7,8},{8,9},{9,10},{10,1... | collective-permute-start | bytes 491528 | tf_op jit(solution)/shard_map/ppermute | solution.py:597
  22.3 1.9 %collective-permute-start.3 = (f32[4,80,128]{2,1,0:T(8,128)S(1)}, f32[4,80,128]{2,1,0:T(8,128)S(1)}, u32[]{:S(2)}, u32[]{:S(2)}) collective-permute-start(f32[4,80,128]{2,1,0:T(8,128)S(1)} %get-tuple-element.18), channel_id=1, source_target_pairs={{1,0},{2,1},{3,2},{4,3},{5,4},{6,5},{7,6},{8,7},{9,8},{10,9},{11,1... | collective-permute-start | bytes 491528 | tf_op jit(solution)/shard_map/ppermute | solution.py:597
  24.2 2.2 %middle.1 = (f32[4,512,512]{2,1,0:T(8,128)}, f32[4,2,272,128]{3,2,1,0:T(8,128)S(1)}) custom-call(f32[4,5,544,128]{3,2,1,0:T(8,128)S(1)} %get-tuple-element.12.outer_ref, f32[4,5,288,128]{3,2,1,0:T(8,128)S(1)} %inner.1.inner_ref, f32[4,5,24,128]{3,2,1,0:T(8,128)S(1)} %get-tuple-element.15.top_ref, f32[4,5,24,128]{3,2,1,0:T(8,128)S(1)} %get-tuple-element.16.bottom_ref, ...), custom_call_target="tpu_custom_call" | custom-call | flops 4000000000 | bytes 4000000 | tf_op jit(solution)/shard_map/middle/pallas_call | solution.py:650
  26.4 0.2 collective-permute-done.2.from_left_ref
  26.6 6.7 %collective-permute-done.3.from_right_ref = f32[4,80,128]{2,1,0:T(8,128)S(1)} collective-permute-done((f32[4,80,128]{2,1,0:T(8,128)S(1)}, f32[4,80,128]{2,1,0:T(8,128)S(1)}, u32[]{:S(2)}, u32[]{:S(2)}) %collective-permute-start.3) | collective-permute-done | bytes 163872 | tf_op jit(solution)/shard_map/ppermute | solution.py:597
  33.3 5.8 %levels.1 = (f32[4,512,512]{2,1,0:T(8,128)}, f32[4,256,256]{2,1,0:T(8,128)}, f32[4,128,128]{2,1,0:T(8,128)}) custom-call(f32[4,5,544,128]{3,2,1,0:T(8,128)S(1)} %get-tuple-element.12.outer_ref, f32[4,5,288,128]{3,2,1,0:T(8,128)S(1)} %inner.1.inner_ref, f32[4,5,24,128]{3,2,1,0:T(8,128)S(1)} %get-tuple-element.15.top_ref, ...), custom_call_target="tpu_custom_call", output_to_operand_aliasing={{0}: (8, {})} | custom-call | tf_op jit(solution)/shard_map/levels/pallas_call | solution.py:665
Async XLA Ops:
  6.3 7.6 %collective-permute-start = (f32[4,5,24,128]{3,2,1,0:T(8,128)S(1)}, f32[4,5,24,128]{3,2,1,0:T(8,128)S(1)}, u32[]{:S(2)}, u32[]{:S(2)}) collective-permute-start(f32[4,5,24,128]{3,2,1,0:T(8,128)S(1)} %get-tuple-element.13), channel_id=1, source_target_pairs={{0,16},{16,32},{32,48},{48,64},{64,80},{80,96},{96,112},{1,17},{17... | collective-permute-start | bytes 737288 | tf_op jit(solution)/shard_map/ppermute | solution.py:597
  9.2 6.3 %collective-permute-start.1 = (f32[4,5,24,128]{3,2,1,0:T(8,128)S(1)}, f32[4,5,24,128]{3,2,1,0:T(8,128)S(1)}, u32[]{:S(2)}, u32[]{:S(2)}) collective-permute-start(f32[4,5,24,128]{3,2,1,0:T(8,128)S(1)} %get-tuple-element.14), channel_id=1, source_target_pairs={{16,0},{32,16},{48,32},{64,48},{80,64},{96,80},{112,96},{17,1},{33... | collective-permute-start | bytes 737288 | tf_op jit(solution)/shard_map/ppermute | solution.py:597
  16.9 9.7 %collective-permute-start.2 = (f32[4,80,128]{2,1,0:T(8,128)S(1)}, f32[4,80,128]{2,1,0:T(8,128)S(1)}, u32[]{:S(2)}, u32[]{:S(2)}) collective-permute-start(f32[4,80,128]{2,1,0:T(8,128)S(1)} %get-tuple-element.17), channel_id=1, source_target_pairs={{0,1},{1,2},{2,3},{3,4},{4,5},{5,6},{6,7},{7,8},{8,9},{9,10},{10,1... | collective-permute-start | bytes 491528 | tf_op jit(solution)/shard_map/ppermute | solution.py:597
  22.3 11.0 %collective-permute-start.3 = (f32[4,80,128]{2,1,0:T(8,128)S(1)}, f32[4,80,128]{2,1,0:T(8,128)S(1)}, u32[]{:S(2)}, u32[]{:S(2)}) collective-permute-start(f32[4,80,128]{2,1,0:T(8,128)S(1)} %get-tuple-element.18), channel_id=1, source_target_pairs={{1,0},{2,1},{3,2},{4,3},{5,4},{6,5},{7,6},{8,7},{9,8},{10,9},{11,1... | collective-permute-start | bytes 491528 | tf_op jit(solution)/shard_map/ppermute | solution.py:597

commit v2 on v1

--- a/solution.py
+++ b/solution.py
@@ -20,6 +20,8 @@
 BAND = 18
 GROUPS = 7
 PACK = 80
+FLAG_ROW = 64
+FLAG_LANE = 108
 XPAD = 24
 CPAD = 8
 CROWS = 560
@@ -65,6 +67,14 @@
     left = taper(x - 2 * (lane[:, None] - 128)).sum(axis=1, dtype=np.float64)
     cols = np.stack([main, np.where(lane >= 64, left, 0.0), np.where(lane < 64, right, 0.0)])
     return (cols[:, None, :] * rows[None, :, None]).astype(np.float32)
+
+
+def band_opacity():
+    main, left, right = opacity_patch()
+    lane = np.arange(128)
+    from_left = np.where(lane >= 113, main, np.where(lane < 3, right, 0.0))
+    from_right = np.where(lane < 15, main, np.where(lane >= 125, left, 0.0))
+    return np.stack([from_left, from_right]).astype(np.float32)
 
 
 def wide_weights(own):
@@ -320,7 +330,7 @@
         return start
 
     sides = ((left_ref, 0, 3), (right_ref, 3, 15))
-    for c in range(4):
+    for c in range(3):
         for out_ref, block, first in sides:
             out_ref[c] = packed(c, block, first, range(1, GROUPS - 1), None)
     for copy in bands:
@@ -329,9 +339,17 @@
         for b in range(5):
             top_ref[c, b] = outer_ref[c, b, 0:TOP, :] + band_ref[0, c, b]
             bottom_ref[c, b] = outer_ref[c, b, ROWS - TOP : ROWS, :] + band_ref[1, c, b]
-    for c in range(4):
+    for c in range(3):
         for out_ref, block, first in sides:
             out_ref[c] = packed(c, block, first, (0, GROUPS - 1), out_ref[c])
+    for out_ref, block, _ in sides:
+        shown = [top_ref[3, block, 6:7, :]]
+        for start in (76, 204, 332, 460):
+            shown.append(canvas_rows(outer_ref, inner_ref, 3, block, start, 1, 128 <= start < 416))
+        shown.append(bottom_ref[3, block, 16:17, :])
+        for i, value in enumerate(shown):
+            row = slice(FLAG_ROW + i, FLAG_ROW + i + 1)
+            out_ref[0, row, :] = jnp.where(lane >= FLAG_LANE, value, out_ref[0, row, :])
 
 
 def finish(linear):
@@ -387,9 +405,11 @@
 STEPS3 = 17
 
 
-def middle_kernel(outer_ref, inner_ref, top_ref, bottom_ref, own_hbm, one_out, part_ref, carried_ref, one_ref, own_ref, sem):
+def middle_kernel(outer_ref, inner_ref, top_ref, bottom_ref, own_hbm, table_hbm, one_out, part_ref, table_ref, carried_ref, one_ref, own_ref, sem):
     load = pltpu.make_async_copy(own_hbm, own_ref, sem.at[2])
     load.start()
+    table_load = pltpu.make_async_copy(table_hbm, table_ref, sem.at[3])
+    table_load.start()
     clear_carried(carried_ref, 2)
 
     def finish_one(row, n, band, band_row, mask, out_row, kind):
@@ -419,6 +439,7 @@
     ]
     level_one_rows(top_ref, bottom_ref, finish_one, copies)
     load.wait()
+    table_load.wait()
 
     def reduce_two(c, carry):
         parts = [
@@ -438,7 +459,7 @@
 
 
 def levels_kernel(
-    outer_ref, inner_ref, top_ref, bottom_ref, from_left_ref, from_right_ref, part_ref, own_hbm, one_in,
+    outer_ref, inner_ref, top_ref, bottom_ref, from_left_ref, from_right_ref, part_ref, table_ref, own_hbm, one_in,
     one_out, two_out, three_out,
     add_ref, carried_ref, linear_ref, carried2_ref, one_ref, two_ref, three_stage, w_ref, sem,
 ):
@@ -455,12 +476,26 @@
 
     from_left_lanes = (lane >= 113) | (lane < 3)
     from_right_lanes = (lane >= 125) | (lane < 15)
-    for c in range(4):
+    for c in range(3):
         for side, ref, first, lanes in ((0, from_left_ref, 15, from_left_lanes), (1, from_right_ref, 3, from_right_lanes)):
             for g in range(GROUPS):
                 start, stop = g * PACK, min(g * PACK + PACK, ROWS)
                 band = pltpu.roll(ref[c, 0 : stop - start, :], (-first - BAND * g) % 128, 1)
                 add_ref[side, c, start:stop, :] = jnp.where(lanes, band, 0.0)
+
+    for side, ref in ((0, from_left_ref), (1, from_right_ref)):
+        flags = [
+            jnp.where(ref[0, FLAG_ROW + i : FLAG_ROW + i + 1, FLAG_LANE : FLAG_LANE + 1] > 0.5, 1.0, 0.0) for i in range(6)
+        ]
+        flags = [jnp.broadcast_to(flag, (8, 128)) for flag in flags]
+        for start in range(0, ROWS, 8):
+            total = None
+            for i in range(6):
+                row = start - 128 * (i - 1) - 8
+                if 0 <= row < PATCH:
+                    term = table_ref[side, row : row + 8, :] * flags[i]
+                    total = term if total is None else total + term
+            add_ref[side, 3, start : start + 8, :] = total
 
     def finish_one(row, n, band, band_row, mask, out_row, kind):
         rows = pl.ds(row, n)
@@ -600,7 +635,7 @@
 def per_device(tiles, slot_tile):
     shape = jax.ShapeDtypeStruct
     band_shape = pltpu.VMEM((4, 5, TOP, 128), F32)
-    pack_shape = pltpu.VMEM((4, PACK, 128), F32)
+    pack_shape = pltpu.VMEM((3, PACK, 128), F32)
     in_hbm = lambda value: pltpu.with_memory_space_constraint(value, pltpu.HBM)
     weights, patch = in_hbm(jnp.asarray(tile_weights())), in_hbm(jnp.asarray(opacity_patch()))
     data, slots = in_hbm(tiles[0]), in_hbm(slot_tile)
@@ -647,26 +682,30 @@
     from_right = shifted(to_left, "col", -1)
     from_left = shifted(to_right, "col", 1)
     middle, rest = level_two_weights()
-    level_one, part = pl.pallas_call(
+    level_one, part, table = pl.pallas_call(
         middle_kernel,
         name="middle",
-        out_shape=(shape((4, 512, 512), F32), pltpu.VMEM((4, 2, ROWS2, 128), F32)),
-        in_specs=[VMEM, VMEM, VMEM, VMEM, HBM],
-        out_specs=(HBM, VMEM),
+        out_shape=(
+            shape((4, 512, 512), F32),
+            pltpu.VMEM((4, 2, ROWS2, 128), F32),
+            pltpu.VMEM((2, PATCH, 128), F32),
+        ),
+        in_specs=[VMEM] * 4 + [HBM] * 2,
+        out_specs=(HBM, VMEM, VMEM),
         scratch_shapes=[
             pltpu.VMEM((4, 2, CROWS, 128), F32),
             pltpu.VMEM((4, 512, 256), F32),
             pltpu.VMEM((2, 256, 256), BF16),
-            pltpu.SemaphoreType.DMA((3,)),
+            pltpu.SemaphoreType.DMA((4,)),
         ],
         cost_estimate=pl.CostEstimate(flops=4_000_000_000, bytes_accessed=4_000_000, transcendentals=0),
         compiler_params=params(30),
-    )(outer, inner, top, bottom, in_hbm(jnp.asarray(middle)))
+    )(outer, inner, top, bottom, in_hbm(jnp.asarray(middle)), in_hbm(jnp.asarray(band_opacity())))
     return pl.pallas_call(
         levels_kernel,
         name="levels",
         out_shape=(shape((4, 512, 512), F32), shape((4, 256, 256), F32), shape((4, 128, 128), F32)),
-        in_specs=[VMEM] * 7 + [HBM, HBM],
+        in_specs=[VMEM] * 8 + [HBM] * 2,
         out_specs=(HBM, HBM, HBM),
         scratch_shapes=[
             pltpu.VMEM((2, 4, ROWS, 128), F32),
@@ -679,9 +718,9 @@
             pltpu.VMEM((8, 256, 256), BF16),
             pltpu.SemaphoreType.DMA((7,)),
         ],
-        input_output_aliases={8: 0},
+        input_output_aliases={9: 0},
         compiler_params=params(30),
-    )(outer, inner, top, bottom, from_left, from_right, part, in_hbm(jnp.asarray(rest)), level_one)
+    )(outer, inner, top, bottom, from_left, from_right, part, table, in_hbm(jnp.asarray(rest)), level_one)
 
 
 def solution(mesh):

time: 39.2 us -> 38 us (0.969)
  the two profiles are of different devices: /device:TPU:70 before, /device:TPU:54 now
where the time goes in v2:
time: 38 us; the launch traced here: 37.9 us
  Pallas kernels  19.7 us (52%)
  starting transfers between devices  11.5 us (30%)
  waiting for transfers between devices  5.9 us (16%)
  between operations  0.71 us (2%)
    ppermute x4, starting transfers between devices, shifted(): return lax.ppermute(value, axis, pairs)  11.5 us
    pallas_call x1, Pallas kernels, per_device(): pl.pallas_call(outer_kernel, name='outer', out_shape=(pltpu.VMEM((4, 5, R...  7.1 us
    ppermute x4, waiting for transfers between devices, shifted(): return lax.ppermute(value, axis, pairs)  5.9 us
    pallas_call x1, Pallas kernels, per_device(): pl.pallas_call(levels_kernel, name='levels', out_shape=(shape((4, 512, 51...  5.62 us
    pallas_call x1, Pallas kernels, per_device(): pl.pallas_call(inner_kernel, name='inner', out_shape=pltpu.VMEM((4, 5, IN...  3.57 us
    pallas_call x1, Pallas kernels, per_device(): pl.pallas_call(middle_kernel, name='middle', out_shape=(shape((4, 512, 51...  2.21 us
    pallas_call x1, Pallas kernels, per_device(): pl.pallas_call(pack_kernel, name='pack', out_shape=(pack_shape, pack_shap...  1.24 us
  transfers between devices with their start and end apart: 4, of which 2 were waited for; matrix products, arithmetic and copies ran while one was open for 0% of the time, Pallas kernels for 15%

profile of v2, /device:TPU:54, one launch (start us, length us, event | category | flops | bytes accessed | tf_op | source)
XLA Modules:
  0.0 37.9 jit_solution(11127542883547889015)
XLA Ops:
  0.6 7.1 %outer.1 = (f32[4,5,544,128]{3,2,1,0:T(8,128)S(1)}, f32[4,5,24,128]{3,2,1,0:T(8,128)S(1)}, f32[4,5,24,128]{3,2,1,0:T(8,128)S(1)}) custom-call(s32[1,12]{1,0:T(1,128)} %slot_ref.3, f32[12,3,256,256]{3,2,1,0:T(8,128)} %bitcast.1, bf16[3,256,256]{2,1,0:T(8,128)(2,1)} %constant.10.clone.weight_ref, f32[3,144,128]{2,1,0:T(8,128)} %constant.11.clone.patch_ref), custom_call_target="tpu_custom_call" | custom-call | tf_op jit(solution)/shard_map/outer/pallas_call | solution.py:652
  7.7 1.9 %collective-permute-start = (f32[4,5,24,128]{3,2,1,0:T(8,128)S(1)}, f32[4,5,24,128]{3,2,1,0:T(8,128)S(1)}, u32[]{:S(2)}, u32[]{:S(2)}) collective-permute-start(f32[4,5,24,128]{3,2,1,0:T(8,128)S(1)} %get-tuple-element.14), channel_id=1, source_target_pairs={{0,16},{16,32},{32,48},{48,64},{64,80},{80,96},{96,112},{1,17},{17... | collective-permute-start | bytes 737288 | tf_op jit(solution)/shard_map/ppermute | solution.py:632
  9.7 3.6 %collective-permute-start.1 = (f32[4,5,24,128]{3,2,1,0:T(8,128)S(1)}, f32[4,5,24,128]{3,2,1,0:T(8,128)S(1)}, u32[]{:S(2)}, u32[]{:S(2)}) collective-permute-start(f32[4,5,24,128]{3,2,1,0:T(8,128)S(1)} %get-tuple-element.15), channel_id=1, source_target_pairs={{16,0},{32,16},{48,32},{64,48},{80,64},{96,80},{112,96},{17,1},{33... | collective-permute-start | bytes 737288 | tf_op jit(solution)/shard_map/ppermute | solution.py:632
  13.3 3.6 %inner.1.inner_ref = f32[4,5,288,128]{3,2,1,0:T(8,128)S(1)} custom-call(s32[1,12]{1,0:T(1,128)} %slot_ref.3, f32[12,3,256,256]{3,2,1,0:T(8,128)} %bitcast.2, bf16[3,256,256]{2,1,0:T(8,128)(2,1)} %constant.10.clone.weight_ref, f32[3,144,128]{2,1,0:T(8,128)} %constant.11.clone.patch_ref), custom_call_target="tpu_custom_call" | custom-call | flops 4000000000 | bytes 4000000 | tf_op jit(solution)/shard_map/inner/pallas_call | solution.py:663
  16.9 0.0 collective-permute-done.above_any
  16.9 0.1 collective-permute-done.1.below_any
  17.0 1.2 %pack.1 = (f32[3,80,128]{2,1,0:T(8,128)S(1)}, f32[3,80,128]{2,1,0:T(8,128)S(1)}, f32[4,5,24,128]{3,2,1,0:T(8,128)S(1)}, f32[4,5,24,128]{3,2,1,0:T(8,128)S(1)}) custom-call(f32[4,5,544,128]{3,2,1,0:T(8,128)S(1)} %get-tuple-element.13.outer_ref, f32[4,5,288,128]{3,2,1,0:T(8,128)S(1)} %inner.1.inner_ref, f32[4,5,24,128]{3,2,1,0:T(8,128)S(1)} %collective-permute-done.above_any, ...), custom_call_target="tpu_custom_call" | custom-call | tf_op jit(solution)/shard_map/pack/pallas_call | solution.py:673
  18.3 4.1 %collective-permute-start.2 = (f32[3,80,128]{2,1,0:T(8,128)S(1)}, f32[3,80,128]{2,1,0:T(8,128)S(1)}, u32[]{:S(2)}, u32[]{:S(2)}) collective-permute-start(f32[3,80,128]{2,1,0:T(8,128)S(1)} %get-tuple-element.18), channel_id=1, source_target_pairs={{0,1},{1,2},{2,3},{3,4},{4,5},{5,6},{6,7},{7,8},{8,9},{9,10},{10,1... | collective-permute-start | bytes 368648 | tf_op jit(solution)/shard_map/ppermute | solution.py:632
  22.3 1.9 %collective-permute-start.3 = (f32[3,80,128]{2,1,0:T(8,128)S(1)}, f32[3,80,128]{2,1,0:T(8,128)S(1)}, u32[]{:S(2)}, u32[]{:S(2)}) collective-permute-start(f32[3,80,128]{2,1,0:T(8,128)S(1)} %get-tuple-element.19), channel_id=1, source_target_pairs={{1,0},{2,1},{3,2},{4,3},{5,4},{6,5},{7,6},{8,7},{9,8},{10,9},{11,1... | collective-permute-start | bytes 368648 | tf_op jit(solution)/shard_map/ppermute | solution.py:632
  24.3 2.2 %middle.1 = (f32[4,512,512]{2,1,0:T(8,128)}, f32[4,2,272,128]{3,2,1,0:T(8,128)S(1)}, f32[2,144,128]{2,1,0:T(8,128)S(1)}) custom-call(f32[4,5,544,128]{3,2,1,0:T(8,128)S(1)} %get-tuple-element.13.outer_ref, f32[4,5,288,128]{3,2,1,0:T(8,128)S(1)} %inner.1.inner_ref, f32[4,5,24,128]{3,2,1,0:T(8,128)S(1)} %get-tuple-element.16.top_ref, ...), custom_call_target="tpu_custom_call" | custom-call | flops 4000000000 | bytes 4000000 | tf_op jit(solution)/shard_map/middle/pallas_call | solution.py:685
  26.5 0.0 collective-permute-done.2.from_left_ref
  26.5 5.8 %collective-permute-done.3.from_right_ref = f32[3,80,128]{2,1,0:T(8,128)S(1)} collective-permute-done((f32[3,80,128]{2,1,0:T(8,128)S(1)}, f32[3,80,128]{2,1,0:T(8,128)S(1)}, u32[]{:S(2)}, u32[]{:S(2)}) %collective-permute-start.3) | collective-permute-done | bytes 122912 | tf_op jit(solution)/shard_map/ppermute | solution.py:632
  32.3 5.6 %levels.1 = (f32[4,512,512]{2,1,0:T(8,128)}, f32[4,256,256]{2,1,0:T(8,128)}, f32[4,128,128]{2,1,0:T(8,128)}) custom-call(f32[4,5,544,128]{3,2,1,0:T(8,128)S(1)} %get-tuple-element.13.outer_ref, f32[4,5,288,128]{3,2,1,0:T(8,128)S(1)} %inner.1.inner_ref, f32[4,5,24,128]{3,2,1,0:T(8,128)S(1)} %get-tuple-element.16.top_ref, ...), custom_call_target="tpu_custom_call", output_to_operand_aliasing={{0}: (9, {})} | custom-call | tf_op jit(solution)/shard_map/levels/pallas_call | solution.py:704
Async XLA Ops:
  7.7 9.2 %collective-permute-start = (f32[4,5,24,128]{3,2,1,0:T(8,128)S(1)}, f32[4,5,24,128]{3,2,1,0:T(8,128)S(1)}, u32[]{:S(2)}, u32[]{:S(2)}) collective-permute-start(f32[4,5,24,128]{3,2,1,0:T(8,128)S(1)} %get-tuple-element.14), channel_id=1, source_target_pairs={{0,16},{16,32},{32,48},{48,64},{64,80},{80,96},{96,112},{1,17},{17... | collective-permute-start | bytes 737288 | tf_op jit(solution)/shard_map/ppermute | solution.py:632
  9.7 7.3 %collective-permute-start.1 = (f32[4,5,24,128]{3,2,1,0:T(8,128)S(1)}, f32[4,5,24,128]{3,2,1,0:T(8,128)S(1)}, u32[]{:S(2)}, u32[]{:S(2)}) collective-permute-start(f32[4,5,24,128]{3,2,1,0:T(8,128)S(1)} %get-tuple-element.15), channel_id=1, source_target_pairs={{16,0},{32,16},{48,32},{64,48},{80,64},{96,80},{112,96},{17,1},{33... | collective-permute-start | bytes 737288 | tf_op jit(solution)/shard_map/ppermute | solution.py:632
  18.3 8.2 %collective-permute-start.2 = (f32[3,80,128]{2,1,0:T(8,128)S(1)}, f32[3,80,128]{2,1,0:T(8,128)S(1)}, u32[]{:S(2)}, u32[]{:S(2)}) collective-permute-start(f32[3,80,128]{2,1,0:T(8,128)S(1)} %get-tuple-element.18), channel_id=1, source_target_pairs={{0,1},{1,2},{2,3},{3,4},{4,5},{5,6},{6,7},{7,8},{8,9},{9,10},{10,1... | collective-permute-start | bytes 368648 | tf_op jit(solution)/shard_map/ppermute | solution.py:632
  22.3 9.9 %collective-permute-start.3 = (f32[3,80,128]{2,1,0:T(8,128)S(1)}, f32[3,80,128]{2,1,0:T(8,128)S(1)}, u32[]{:S(2)}, u32[]{:S(2)}) collective-permute-start(f32[3,80,128]{2,1,0:T(8,128)S(1)} %get-tuple-element.19), channel_id=1, source_target_pairs={{1,0},{2,1},{3,2},{4,3},{5,4},{6,5},{7,6},{8,7},{9,8},{10,9},{11,1... | collective-permute-start | bytes 368648 | tf_op jit(solution)/shard_map/ppermute | solution.py:632
